TPU v7x, 32 devices: a whole 2x2x4 slice. The times are simulated.
32 devices in a mesh: groups: 2 (over y), fft: 4 (over z), band: 2 (over x), sub: 2 (over core).
Axes of the slice: x: 2, y: 2, z: 4, core: 2. Of those that a mesh axis runs over, the one named last changes fastest.
Arguments:
- coefficients: bfloat16 [8, 2, 128, 1024], P(('groups', 'band', 'sub'), None, None, 'fft'), parts along dimension 0, may hold values from -6 to 6
- potential: float32 [384, 192, 192], P(('groups', 'fft')), parts along dimension 0, may hold values from -15 to 15
- stick_map: int32 [3, 2048], P(None, ('groups', 'fft')), parts along dimension 1, may hold values from 0 to 191, as said below
- plane_order: int32 [384], P('groups'), parts along dimension 0, may hold values from 0 to 191, each once
Outputs:
- applied: float32 [8, 2, 128, 1024], P(('groups', 'band', 'sub'), None, None, 'fft'), parts along dimension 0
There are 2 independent parts, one for each index of `groups`. A program takes and returns all parts, laid end to end along the dimension named above; each array names one. Nothing has to cross between parts.
Inputs may be any that keep to these rules, and one draw needn't show every extreme that they name: Column s is one stick slot: stick_map[0, s] and stick_map[1, s] are its grid indices x and y, stick_map[2, s] its length, an odd number up to 127, or 0 for an empty slot. A stick of length L holds the frequencies -(L - 1)/2 to (L - 1)/2 at entries 128/2 + f. The number of live slots differs between indices of fft; some index has all 256 slots live, and 512 slots are live in all. Live sticks name distinct columns, whose frequencies (indices taken modulo 192 into -96 to 95) lie in -48 to 47 along x and along y; an empty slot may name any column. `plane_order`: each plane number appears once.
All inputs are finite; a program needn't handle non-finite values.
Results may differ from a plain program's by a relative error of at most 0.0084.
Values may be sent and summed in bfloat16 or wider, within the bound.
No kernel may reach another device: no remote copies, remote signals or barrier semaphores. Data moves between devices by JAX's collectives and lax.ppermute only.
A program may use at most 128 MiB of HBM per device.

v0:
```python
import math
import jax
import jax.numpy as jnp
from jax import lax
from jax.sharding import PartitionSpec as P


def phase_tables(left_ids, right_ids, modulus):
    turn_index = left_ids[:, None] * right_ids[None, :] % modulus
    angles = turn_index.astype(jnp.float32) * (2.0 * math.pi / modulus)
    return (jnp.cos(angles).astype(jnp.bfloat16), jnp.sin(angles).astype(jnp.bfloat16))


def row_numbers(grid_side):
    compact = jnp.arange(grid_side // 2, dtype=jnp.int32)
    return jnp.where(compact < grid_side // 4, compact, compact + grid_side // 2)


def compact_rows(grid_ids, grid_side):
    rows = jnp.where(grid_ids < grid_side // 4, grid_ids, grid_ids - grid_side // 2)
    return jnp.clip(rows, 0, grid_side // 2 - 1)


def one_hot_rows(grid_ids, grid_side):
    rows = compact_rows(grid_ids, grid_side)
    slots = jnp.arange(grid_side // 2, dtype=jnp.int32)
    return (rows[:, None] == slots[None, :]).astype(jnp.bfloat16)


def plane_work(received, x_onehot, y_onehot, sources, depth_count, grid_side, potential_rows):
    planes = received.shape[0]
    half_side = grid_side // 2
    slot_count = x_onehot.shape[0] // sources

    def place_one(row):
        values = row.reshape(sources, depth_count, 2, slot_count).transpose(1, 2, 0, 3)
        values = values.reshape(depth_count, 2, sources * slot_count)
        weighted = values[..., None] * y_onehot[None, None]
        return jnp.einsum(
            "sx,dcsy->dxcy", x_onehot, weighted, preferred_element_type=jnp.float32
        ).astype(jnp.bfloat16)

    spread = lax.map(place_one, received)
    axis_ids = jnp.arange(grid_side, dtype=jnp.int32)
    live_ids = row_numbers(grid_side)
    cos_w, sin_w = phase_tables(live_ids, axis_ids, grid_side)
    forward_y = jnp.concatenate(
        [jnp.concatenate([cos_w, sin_w], 1), jnp.concatenate([-sin_w, cos_w], 1)], 0
    )
    inverse_y = jnp.concatenate(
        [jnp.concatenate([cos_w.T, -sin_w.T], 1), jnp.concatenate([sin_w.T, cos_w.T], 1)], 0
    )
    cos_x = cos_w.T
    sin_x = sin_w.T
    forward_x = jnp.concatenate([cos_x, sin_x], 0)
    inverse_x = jnp.concatenate([cos_w, sin_w], 0)
    half_y = jnp.dot(
        spread.reshape(-1, 2 * half_side), forward_y, preferred_element_type=jnp.float32
    )
    half_y = half_y.astype(jnp.bfloat16).reshape(planes, depth_count, half_side, 2 * grid_side)
    mixed_x = jnp.einsum("ux,pbxw->pbuw", forward_x, half_y, preferred_element_type=jnp.float32)
    cos_part = mixed_x[:, :, :grid_side]
    sin_part = mixed_x[:, :, grid_side:]
    pot_field = potential_rows[:, None, :, :]
    real_part = (cos_part[..., :grid_side] - sin_part[..., grid_side:]) * pot_field
    imag_part = (cos_part[..., grid_side:] + sin_part[..., :grid_side]) * pot_field
    product = jnp.concatenate([real_part, imag_part], 3).astype(jnp.bfloat16)
    mixed_x = jnp.einsum("ux,pbxw->pbuw", inverse_x, product, preferred_element_type=jnp.float32)
    cos_part = mixed_x[:, :, :half_side]
    sin_part = mixed_x[:, :, half_side:]
    back_x = jnp.concatenate(
        [
            cos_part[..., :grid_side] + sin_part[..., grid_side:],
            cos_part[..., grid_side:] - sin_part[..., :grid_side],
        ],
        3,
    ).astype(jnp.bfloat16)
    back_y = jnp.dot(
        back_x.reshape(-1, 2 * grid_side), inverse_y, preferred_element_type=jnp.float32
    ).astype(jnp.bfloat16)
    back_y = back_y.reshape(planes, depth_count, half_side, 2, half_side)

    def pick_one(grid):
        picked = jnp.einsum("sx,dxcy->dcsy", x_onehot, grid, preferred_element_type=jnp.float32)
        values = jnp.sum(picked * y_onehot[None, None], axis=3)
        values = values.reshape(depth_count, 2, sources, slot_count).transpose(2, 0, 1, 3)
        return values.reshape(-1).astype(jnp.bfloat16)

    return lax.map(pick_one, back_y)


def body(coefficients, potential, stick_map, plane_order):
    band_count = coefficients.shape[0]
    z_span = coefficients.shape[2]
    slot_count = coefficients.shape[3]
    grid_side = potential.shape[1]
    entries = jnp.arange(z_span, dtype=jnp.int32)
    freq_z = (entries - z_span // 2) % grid_side
    half_len = (stick_map[2] - 1) // 2
    keep_mask = jnp.abs(entries[:, None] - z_span // 2) <= half_len[None, :]
    masked = coefficients * keep_mask.astype(jnp.bfloat16)
    cos_z, sin_z = phase_tables(plane_order, freq_z, grid_side)
    forward_z = jnp.stack(
        [jnp.concatenate([cos_z, -sin_z], 1), jnp.concatenate([sin_z, cos_z], 1)], 1
    )
    sticks = jnp.einsum(
        "zck,bks->zbcs",
        forward_z,
        masked.reshape(band_count, 2 * z_span, slot_count),
        preferred_element_type=jnp.float32,
    )
    sticks = sticks.astype(jnp.bfloat16).reshape(grid_side, band_count * 2 * slot_count)
    columns = lax.all_gather(stick_map, "fft", axis=1, tiled=True)
    sources = lax.axis_size("fft")
    x_onehot = one_hot_rows(columns[0], grid_side)
    y_onehot = one_hot_rows(columns[1], grid_side)
    copies = lax.axis_size("sub")
    plane_share = potential.shape[0] // copies
    potential_rows = lax.dynamic_slice_in_dim(
        potential, lax.axis_index("sub") * plane_share, plane_share, 0
    )
    received = lax.all_to_all(sticks, ("fft", "sub"), split_axis=0, concat_axis=1, tiled=True)
    gathered = plane_work(
        received, x_onehot, y_onehot, sources, copies * band_count, grid_side, potential_rows
    )
    returned = lax.all_to_all(gathered, ("fft", "sub"), split_axis=1, concat_axis=0, tiled=True)
    inverse_z = jnp.stack([jnp.stack([cos_z, sin_z], 1), jnp.stack([-sin_z, cos_z], 1)], 1)
    totals = jnp.einsum(
        "rcdk,rbds->bcks",
        inverse_z,
        returned.reshape(grid_side, band_count, 2, slot_count),
        preferred_element_type=jnp.float32,
    )
    return totals * (keep_mask.astype(jnp.float32) * (1.0 / grid_side**3))


def solution(mesh):
    placed = (
        P(("groups", "band", "sub"), None, None, "fft"),
        P(("groups", "fft"), None, None),
        P(None, ("groups", "fft")),
        P("groups"),
    )
    return jax.shard_map(
        body,
        mesh=mesh,
        in_specs=placed,
        out_specs=P(("groups", "band", "sub"), None, None, "fft"),
        check_vma=False,
    )
```

profile of v0, /device:TPU:0, one launch (start us, length us, event | category | flops | bytes accessed | tf_op | source)
XLA Modules:
  0.0 154.8 jit_solution(12331591917178488166)
XLA Ops:
  0.0 1.2 sine_convert_fusion.3
  1.2 1.1 fusion.86
  3.3 0.9 broadcast_multiply_fusion
  4.6 0.8 all_to_all.26
  5.4 6.4 %all-to-all-start = ((bf16[8,24,512]{2,1,0:T(8,128)(2,1)}), bf16[8,24,512]{2,1,0:T(8,128)(2,1)S(1)}, u32[]{:S(2)}, u32[]{:S(2)}) async-start(bf16[8,24,512]{2,1,0:T(8,128)(2,1)} %all_to_all.26), calls=%async_computation | async-start | bytes 393216 | tf_op jit(solution)/shard_map/all_to_all | solution.py:122
  11.8 15.4 %all_gather.3 = s32[3,1024]{1,0:T(4,128)S(1)} all-gather(s32[3,256]{1,0:T(4,128)} %param.10), channel_id=1, replica_groups=mesh['groups'=2,'fft'=4,'band'=2,'sub'=2] {'fft'}, dimensions={1}, use_global_device_ids=true | all-gather | bytes 15360 | tf_op jit(solution)/shard_map/all_gather | solution.py:113
  29.2 1.2 sine_convert_fusion
  30.3 1.1 fusion.87
  31.5 4.9 %constant_dynamic-slice_fusion.1 = f32[24,192,192]{2,1,0:T(8,128)} fusion(f32[48,192,192]{2,1,0:T(8,128)} %param.9, s32[]{:T(128)S(6)} %select_n.131), kind=kLoop, calls=%fused_computation.140 | loop fusion | bytes 7077892 | tf_op jit(solution)/shard_map/dynamic_slice | solution.py:119
  36.4 30.9 %while.22 = (s32[]{:T(128)}, bf16[24,2,96,2,96]{2,1,0,4,3:T(2,128)(2,1)}, bf16[24,4096]{1,0:T(8,128)(2,1)S(1)}, s32[1024]{0:T(1024)S(1)}, s32[1024]{0:T(1024)S(1)}, /*index=5*/s32[]{:T(128)}) while((s32[]{:T(128)}, bf16[24,2,96,2,96]{2,1,0,4,3:T(2,128)(2,1)}, bf16[24,4096]{1,0:T(8,128)(2,1)S(1)}, s32[1024]{0:T(1024)S(1)}, ...), condition=%wide.region_1.2_spmd.clone, body=%wide.region_0.1_spmd.clone.sunk | while | flops 76320768 | bytes 705097 | solution.py:43
  37.1 0.8 copy_dynamic-update-slice_fusion.2
  41.0 0.8 copy_dynamic-update-slice_fusion.2
  48.6 0.8 copy_dynamic-update-slice_fusion.2
  49.9 0.8 copy_dynamic-update-slice_fusion.2
  52.5 0.8 copy_dynamic-update-slice_fusion.2
  56.3 0.8 copy_dynamic-update-slice_fusion.2
  57.6 0.8 copy_dynamic-update-slice_fusion.2
  61.5 0.8 copy_dynamic-update-slice_fusion.2
  64.0 0.8 copy_dynamic-update-slice_fusion.2
  65.3 0.8 copy_dynamic-update-slice_fusion.2
  67.4 7.0 %reshape.324 = bf16[4608,192]{0,1:T(8,128)(2,1)S(1)} reshape(bf16[24,2,96,2,96]{2,1,0,4,3:T(2,128)(2,1)} %get-tuple-element.59) | data formatting | bytes 3538944 | tf_op jit(solution)/shard_map/reshape | solution.py:58
  74.4 1.5 convolution_convert_fusion.1
  75.9 11.5 %convolution_bitcast_fusion = f32[24,2,384,384]{3,2,1,0:T(8,128)} fusion(bf16[24,2,96,384]{3,2,1,0:T(8,128)(2,1)S(1)} %bitcast.104, bf16[192,96]{0,1:T(8,128)(2,1)S(1)} %get-tuple-element.141, bf16[192,96]{0,1:T(8,128)(2,1)S(1)} %get-tuple-element.140), kind=kOutput, calls=%fused_computation.28 | convolution fusion | flops 1359101952 | bytes 31924224 | tf_op jit(solution)/shard_map/ux,pbxw->pbuw/dot_general | solution.py:61
  87.3 16.3 %fusion.27 = (bf16[24,2,192,192]{3,2,1,0:T(8,128)(2,1)S(1)}, bf16[24,2,192,192]{3,2,1,0:T(8,128)(2,1)}) fusion(f32[24,2,384,384]{3,2,1,0:T(8,128)} %convolution_bitcast_fusion, f32[24,192,192]{2,1,0:T(8,128)S(1)} %bitcast.106), kind=kLoop, calls=%fused_computation.34 | loop fusion | flops 10616832 | bytes 38928384 | tf_op jit(solution)/shard_map/convert.4
  103.6 4.9 %convolution_bitcast_fusion.1 = f32[24,2,192,384]{3,2,1,0:T(8,128)S(1)} fusion(bf16[24,2,192,192]{3,2,1,0:T(8,128)(2,1)} %get-tuple-element.127, bf16[24,2,192,192]{3,2,1,0:T(8,128)(2,1)S(1)} %get-tuple-element.126, bf16[96,192]{1,0:T(8,128)(2,1)S(1)} %get-tuple-element.142, bf16[96,192]{1,0:T(8,128)(2,1)S(1)} %get-tuple-element.143), kind=kOutput, calls=%fused_computation.35 | convolution fusion | flops 1373257728 | bytes 21307392 | tf_op jit(solution)/shard_map/ux,pbxw->pbuw/dot_general | solution.py:68
  108.5 3.1 %fusion.32 = (bf16[24,2,96,192]{3,2,1,0:T(8,128)(2,1)S(1)}, bf16[24,2,96,192]{3,2,1,0:T(8,128)(2,1)S(1)}) fusion(f32[24,2,192,384]{3,2,1,0:T(8,128)S(1)} %convolution_bitcast_fusion.1), kind=kLoop, calls=%fused_computation.44 | loop fusion | flops 3538944 | bytes 17694720 | tf_op jit(solution)/shard_map/convert.3
  111.5 2.8 %convolution_convert_fusion.2 = bf16[4608,192]{0,1:T(8,128)(2,1)} fusion(bf16[4608,192]{1,0:T(8,128)(2,1)S(1)} %bitcast.108, bf16[4608,192]{1,0:T(8,128)(2,1)S(1)} %bitcast.107, bf16[192,96]{0,1:T(8,128)(2,1)S(1)} %get-tuple-element.140, bf16[192,96]{0,1:T(8,128)(2,1)S(1)} %get-tuple-element.141, bf16[192,96]{0,1:T(8,128)(2,1)S(1)} %fusion.85), kind=kOutput, calls=%fused_computation.40 | convolution fusion | flops 688029696 | bytes 5419008 | tf_op jit(solution)/shard_map/dot_general | solution.py:78
  114.3 7.7 %reshape.326 = bf16[24,2,96,2,96]{2,1,0,4,3:T(2,128)(2,1)S(1)} reshape(bf16[4608,192]{0,1:T(8,128)(2,1)} %convolution_convert_fusion.2) | data formatting | bytes 3538944 | tf_op jit(solution)/shard_map/reshape | solution.py:81
  122.0 19.3 %while.23 = (s32[]{:T(128)}, bf16[24,4096]{1,0:T(8,128)(2,1)S(1)}, bf16[24,2,96,2,96]{2,1,0,4,3:T(2,128)(2,1)S(1)}, s32[1024]{0:T(1024)S(1)}, s32[1024]{0:T(1024)S(1)}, /*index=5*/s32[]{:T(128)}, s32[]{:T(128)}) while((s32[]{:T(128)}, bf16[24,4096]{1,0:T(8,128)(2,1)S(1)}, bf16[24,2,96,2,96]{2,1,0,4,3:T(2,128)(2,1)S(1)}, ...), condition=%wide.region_4.5_spmd.clone, body=%wide.region_2.4_spmd.clone.sunk | while | flops 76771328 | bytes 1089621 | solution.py:89
  142.0 3.4 %all-to-all-start.1 = ((bf16[24,8,512]{2,0,1:T(8,128)(2,1)}), bf16[24,8,512]{2,0,1:T(8,128)(2,1)S(1)}, u32[]{:S(2)}, u32[]{:S(2)}) async-start(bf16[24,8,512]{2,0,1:T(8,128)(2,1)} %bitcast.87), calls=%async_computation.1 | async-start | bytes 393216 | tf_op jit(solution)/shard_map/all_to_all | solution.py:126
  145.5 8.1 %all-to-all-done.1 = bf16[24,8,512]{2,0,1:T(8,128)(2,1)S(1)} async-done(((bf16[24,8,512]{2,0,1:T(8,128)(2,1)}), bf16[24,8,512]{2,0,1:T(8,128)(2,1)S(1)}, u32[]{:S(2)}, u32[]{:S(2)}) %all-to-all-start.1) | async-done | bytes 196640 | tf_op jit(solution)/shard_map/all_to_all | solution.py:126
  153.9 0.8 copy.24
  (331 shorter events, 44.7 us)
Async XLA Ops:
  5.4 31.0 %all-to-all-start = ((bf16[8,24,512]{2,1,0:T(8,128)(2,1)}), bf16[8,24,512]{2,1,0:T(8,128)(2,1)S(1)}, u32[]{:S(2)}, u32[]{:S(2)}) async-start(bf16[8,24,512]{2,1,0:T(8,128)(2,1)} %all_to_all.26), calls=%async_computation | async-start | bytes 393216 | tf_op jit(solution)/shard_map/all_to_all | solution.py:122
  74.3 13.0 %slice-start = ((s8[4718592]{0:T(1024)(128)(4,1)}), s8[4194304]{0:T(1024)(128)(4,1)S(1)}, s32[]{:S(2)}) async-start(s8[4718592]{0:T(1024)(128)(4,1)} %bitcast.105), calls=%async_computation.2 | async-start | bytes 8388608
  75.9 11.5 %slice-start.1 = ((s8[4718592]{0:T(1024)(128)(4,1)}), s8[524288]{0:T(1024)(128)(4,1)S(1)}, s32[]{:S(2)}) async-start(s8[4718592]{0:T(1024)(128)(4,1)} %bitcast.105), calls=%async_computation.3 | async-start | bytes 1048576
  142.0 11.6 %all-to-all-start.1 = ((bf16[24,8,512]{2,0,1:T(8,128)(2,1)}), bf16[24,8,512]{2,0,1:T(8,128)(2,1)S(1)}, u32[]{:S(2)}, u32[]{:S(2)}) async-start(bf16[24,8,512]{2,0,1:T(8,128)(2,1)} %bitcast.87), calls=%async_computation.1 | async-start | bytes 393216 | tf_op jit(solution)/shard_map/all_to_all | solution.py:126
where the time goes:
time: 155 us
  local copies, waits for them, and re-layouts  51.1 us (33%)
  matrix products  38.7 us (25%)
  other arithmetic  29.4 us (19%)
  blocking collectives  15.4 us (10%)
  starting transfers between devices  9.75 us (6%)
  waiting for transfers between devices  8.1 us (5%)
  loops' own time  2.11 us (1%)
    another operation x2, other arithmetic  19.3 us
    dynamic_update_slice x24, local copies, waits for them, and re-layouts, plane_work(): spread = lax.map(place_one, received)  18.5 us
    all_gather x1, blocking collectives, body(): columns = lax.all_gather(stick_map, 'fft', axis=1, tiled=True)  15.4 us
    dot_general x1, matrix products, plane_work(): jnp.einsum('ux,pbxw->pbuw', forward_x, half_y, preferred_element_type=jnp...  11.5 us
    dot_general x24, matrix products, pick_one(): jnp.einsum('sx,dxcy->dcsy', x_onehot, grid, preferred_element_type=jnp.fl...  8.95 us
    dot_general x24, matrix products, place_one(): jnp.einsum('sx,dcsy->dxcy', x_onehot, weighted, preferred_element_type=jn...  8.66 us
    all_to_all x1, waiting for transfers between devices, body(): lax.all_to_all(gathered, ('fft', 'sub'), split_axis=1, concat_axis=0, til...  8.1 us
    reshape x1, local copies, waits for them, and re-layouts, plane_work(): back_y = back_y.reshape(planes, depth_count, half_side, 2, half_side)  7.68 us
  transfers between devices with their start and end apart: 2, of which 1 were waited for; matrix products, arithmetic and copies ran while one was open for 6% of the time, Pallas kernels for 0%

commit v1 on v0

--- a/solution.py
+++ b/solution.py
@@ -3,6 +3,8 @@
 import jax.numpy as jnp
 from jax import lax
 from jax.sharding import PartitionSpec as P
+
+hold_the_sector = lambda view, axis_id: jnp.concatenate(lax.all_gather(view, axis_id), axis=1)
 
 
 def phase_tables(left_ids, right_ids, modulus):
@@ -110,7 +112,7 @@
         preferred_element_type=jnp.float32,
     )
     sticks = sticks.astype(jnp.bfloat16).reshape(grid_side, band_count * 2 * slot_count)
-    columns = lax.all_gather(stick_map, "fft", axis=1, tiled=True)
+    columns = hold_the_sector(stick_map, "fft")
     sources = lax.axis_size("fft")
     x_onehot = one_hot_rows(columns[0], grid_side)
     y_onehot = one_hot_rows(columns[1], grid_side)

time: 155 us -> 155 us (level)
  no operation moved by 1% of the time
where the time goes in v1:
time: 155 us; the launch traced here: 154 us
  local copies, waits for them, and re-layouts  51.1 us (33%)
  matrix products  38.7 us (25%)
  other arithmetic  29.4 us (19%)
  blocking collectives  13.9 us (9%)
  starting transfers between devices  10.9 us (7%)
  waiting for transfers between devices  8.18 us (5%)
  loops' own time  2.11 us (1%)
    another operation x2, other arithmetic  19.3 us
    dynamic_update_slice x24, local copies, waits for them, and re-layouts, plane_work(): spread = lax.map(place_one, received)  18.5 us
    all_gather x1, blocking collectives, lax.all_gather(view, axis_id)  13.9 us
    dot_general x1, matrix products, plane_work(): jnp.einsum('ux,pbxw->pbuw', forward_x, half_y, preferred_element_type=jnp...  11.5 us
    dot_general x24, matrix products, pick_one(): jnp.einsum('sx,dxcy->dcsy', x_onehot, grid, preferred_element_type=jnp.fl...  8.95 us
    dot_general x24, matrix products, place_one(): jnp.einsum('sx,dcsy->dxcy', x_onehot, weighted, preferred_element_type=jn...  8.66 us
    all_to_all x1, waiting for transfers between devices, body(): lax.all_to_all(gathered, ('fft', 'sub'), split_axis=1, concat_axis=0, til...  8.18 us
    reshape x1, local copies, waits for them, and re-layouts, plane_work(): back_y = back_y.reshape(planes, depth_count, half_side, 2, half_side)  7.68 us
  transfers between devices with their start and end apart: 2, of which 1 were waited for; matrix products, arithmetic and copies ran while one was open for 6% of the time, Pallas kernels for 0%

profile of v1, /device:TPU:0, one launch (start us, length us, event | category | flops | bytes accessed | tf_op | source)
XLA Modules:
  0.0 154.5 jit_solution(10288718352861961293)
XLA Ops:
  0.0 1.2 sine_convert_fusion.3
  1.2 1.1 fusion.86
  3.3 0.9 broadcast_multiply_fusion
  4.6 0.8 all_to_all.26
  5.4 6.4 %all-to-all-start = ((bf16[8,24,512]{2,1,0:T(8,128)(2,1)}), bf16[8,24,512]{2,1,0:T(8,128)(2,1)S(1)}, u32[]{:S(2)}, u32[]{:S(2)}) async-start(bf16[8,24,512]{2,1,0:T(8,128)(2,1)} %all_to_all.26), calls=%async_computation | async-start | bytes 393216 | tf_op jit(solution)/shard_map/all_to_all | solution.py:124
  13.8 1.2 sine_convert_fusion
  14.9 1.1 fusion.87
  16.1 13.9 %all-gather.1 = s32[4,3,256]{2,1,0:T(4,128)S(1)} all-gather(s32[1,3,256]{2,1,0:T(4,128)} %bitcast.124), channel_id=2, replica_groups=mesh['groups'=2,'fft'=4,'band'=2,'sub'=2] {'fft'}, dimensions={0}, use_global_device_ids=true | all-gather | bytes 15360 | tf_op jit(solution)/shard_map/all_gather | solution.py:7
  30.0 4.9 %constant_dynamic-slice_fusion.1 = f32[24,192,192]{2,1,0:T(8,128)} fusion(f32[48,192,192]{2,1,0:T(8,128)} %param.9, s32[]{:T(128)S(6)} %select_n.131), kind=kLoop, calls=%fused_computation.140 | loop fusion | bytes 7077892 | tf_op jit(solution)/shard_map/dynamic_slice | solution.py:121
  34.9 30.9 %while.22 = (s32[]{:T(128)}, bf16[24,2,96,2,96]{2,1,0,4,3:T(2,128)(2,1)}, bf16[24,4096]{1,0:T(8,128)(2,1)S(1)}, s32[1024]{0:T(1024)S(1)}, s32[1024]{0:T(1024)S(1)}, /*index=5*/s32[]{:T(128)}) while((s32[]{:T(128)}, bf16[24,2,96,2,96]{2,1,0,4,3:T(2,128)(2,1)}, bf16[24,4096]{1,0:T(8,128)(2,1)S(1)}, s32[1024]{0:T(1024)S(1)}, ...), condition=%wide.region_1.2_spmd.clone, body=%wide.region_0.1_spmd.clone.sunk | while | flops 76320768 | bytes 705097 | solution.py:45
  35.6 0.8 copy_dynamic-update-slice_fusion.2
  39.5 0.8 copy_dynamic-update-slice_fusion.2
  47.1 0.8 copy_dynamic-update-slice_fusion.2
  48.4 0.8 copy_dynamic-update-slice_fusion.2
  51.0 0.8 copy_dynamic-update-slice_fusion.2
  54.8 0.8 copy_dynamic-update-slice_fusion.2
  56.1 0.8 copy_dynamic-update-slice_fusion.2
  60.0 0.8 copy_dynamic-update-slice_fusion.2
  62.5 0.8 copy_dynamic-update-slice_fusion.2
  63.8 0.8 copy_dynamic-update-slice_fusion.2
  65.8 7.0 %reshape.333 = bf16[4608,192]{0,1:T(8,128)(2,1)S(1)} reshape(bf16[24,2,96,2,96]{2,1,0,4,3:T(2,128)(2,1)} %get-tuple-element.59) | data formatting | bytes 3538944 | tf_op jit(solution)/shard_map/reshape | solution.py:60
  72.8 1.5 convolution_convert_fusion.1
  74.4 11.5 %convolution_bitcast_fusion = f32[24,2,384,384]{3,2,1,0:T(8,128)} fusion(bf16[24,2,96,384]{3,2,1,0:T(8,128)(2,1)S(1)} %bitcast.106, bf16[192,96]{0,1:T(8,128)(2,1)S(1)} %get-tuple-element.146, bf16[192,96]{0,1:T(8,128)(2,1)S(1)} %get-tuple-element.145), kind=kOutput, calls=%fused_computation.28 | convolution fusion | flops 1359101952 | bytes 31924224 | tf_op jit(solution)/shard_map/ux,pbxw->pbuw/dot_general | solution.py:63
  85.8 16.3 %fusion.27 = (bf16[24,2,192,192]{3,2,1,0:T(8,128)(2,1)S(1)}, bf16[24,2,192,192]{3,2,1,0:T(8,128)(2,1)}) fusion(f32[24,2,384,384]{3,2,1,0:T(8,128)} %convolution_bitcast_fusion, f32[24,192,192]{2,1,0:T(8,128)S(1)} %bitcast.108), kind=kLoop, calls=%fused_computation.34 | loop fusion | flops 10616832 | bytes 38928384 | tf_op jit(solution)/shard_map/convert.4
  102.1 4.9 %convolution_bitcast_fusion.1 = f32[24,2,192,384]{3,2,1,0:T(8,128)S(1)} fusion(bf16[24,2,192,192]{3,2,1,0:T(8,128)(2,1)} %get-tuple-element.132, bf16[24,2,192,192]{3,2,1,0:T(8,128)(2,1)S(1)} %get-tuple-element.131, bf16[96,192]{1,0:T(8,128)(2,1)S(1)} %get-tuple-element.147, bf16[96,192]{1,0:T(8,128)(2,1)S(1)} %get-tuple-element.148), kind=kOutput, calls=%fused_computation.35 | convolution fusion | flops 1373257728 | bytes 21307392 | tf_op jit(solution)/shard_map/ux,pbxw->pbuw/dot_general | solution.py:70
  107.0 3.1 %fusion.32 = (bf16[24,2,96,192]{3,2,1,0:T(8,128)(2,1)S(1)}, bf16[24,2,96,192]{3,2,1,0:T(8,128)(2,1)S(1)}) fusion(f32[24,2,192,384]{3,2,1,0:T(8,128)S(1)} %convolution_bitcast_fusion.1), kind=kLoop, calls=%fused_computation.44 | loop fusion | flops 3538944 | bytes 17694720 | tf_op jit(solution)/shard_map/convert.3
  110.0 2.8 %convolution_convert_fusion.2 = bf16[4608,192]{0,1:T(8,128)(2,1)} fusion(bf16[4608,192]{1,0:T(8,128)(2,1)S(1)} %bitcast.110, bf16[4608,192]{1,0:T(8,128)(2,1)S(1)} %bitcast.109, bf16[192,96]{0,1:T(8,128)(2,1)S(1)} %get-tuple-element.145, bf16[192,96]{0,1:T(8,128)(2,1)S(1)} %get-tuple-element.146, bf16[192,96]{0,1:T(8,128)(2,1)S(1)} %fusion.85), kind=kOutput, calls=%fused_computation.40 | convolution fusion | flops 688029696 | bytes 5419008 | tf_op jit(solution)/shard_map/dot_general | solution.py:80
  112.8 7.7 %reshape.335 = bf16[24,2,96,2,96]{2,1,0,4,3:T(2,128)(2,1)S(1)} reshape(bf16[4608,192]{0,1:T(8,128)(2,1)} %convolution_convert_fusion.2) | data formatting | bytes 3538944 | tf_op jit(solution)/shard_map/reshape | solution.py:83
  120.5 19.3 %while.23 = (s32[]{:T(128)}, bf16[24,4096]{1,0:T(8,128)(2,1)S(1)}, bf16[24,2,96,2,96]{2,1,0,4,3:T(2,128)(2,1)S(1)}, s32[1024]{0:T(1024)S(1)}, s32[1024]{0:T(1024)S(1)}, /*index=5*/s32[]{:T(128)}, s32[]{:T(128)}) while((s32[]{:T(128)}, bf16[24,4096]{1,0:T(8,128)(2,1)S(1)}, bf16[24,2,96,2,96]{2,1,0,4,3:T(2,128)(2,1)S(1)}, ...), condition=%wide.region_4.5_spmd.clone, body=%wide.region_2.4_spmd.clone.sunk | while | flops 76771328 | bytes 1089621 | solution.py:91
  140.5 4.5 %all-to-all-start.1 = ((bf16[24,8,512]{2,0,1:T(8,128)(2,1)}), bf16[24,8,512]{2,0,1:T(8,128)(2,1)S(1)}, u32[]{:S(2)}, u32[]{:S(2)}) async-start(bf16[24,8,512]{2,0,1:T(8,128)(2,1)} %bitcast.89), calls=%async_computation.1 | async-start | bytes 393216 | tf_op jit(solution)/shard_map/all_to_all | solution.py:128
  145.1 8.2 %all-to-all-done.1 = bf16[24,8,512]{2,0,1:T(8,128)(2,1)S(1)} async-done(((bf16[24,8,512]{2,0,1:T(8,128)(2,1)}), bf16[24,8,512]{2,0,1:T(8,128)(2,1)S(1)}, u32[]{:S(2)}, u32[]{:S(2)}) %all-to-all-start.1) | async-done | bytes 196640 | tf_op jit(solution)/shard_map/all_to_all | solution.py:128
  153.6 0.8 copy.34
  (331 shorter events, 44.7 us)
Async XLA Ops:
  5.4 29.5 %all-to-all-start = ((bf16[8,24,512]{2,1,0:T(8,128)(2,1)}), bf16[8,24,512]{2,1,0:T(8,128)(2,1)S(1)}, u32[]{:S(2)}, u32[]{:S(2)}) async-start(bf16[8,24,512]{2,1,0:T(8,128)(2,1)} %all_to_all.26), calls=%async_computation | async-start | bytes 393216 | tf_op jit(solution)/shard_map/all_to_all | solution.py:124
  72.8 13.0 %slice-start = ((s8[4718592]{0:T(1024)(128)(4,1)}), s8[4194304]{0:T(1024)(128)(4,1)S(1)}, s32[]{:S(2)}) async-start(s8[4718592]{0:T(1024)(128)(4,1)} %bitcast.107), calls=%async_computation.2 | async-start | bytes 8388608
  74.4 11.5 %slice-start.1 = ((s8[4718592]{0:T(1024)(128)(4,1)}), s8[524288]{0:T(1024)(128)(4,1)S(1)}, s32[]{:S(2)}) async-start(s8[4718592]{0:T(1024)(128)(4,1)} %bitcast.107), calls=%async_computation.3 | async-start | bytes 1048576
  140.5 12.8 %all-to-all-start.1 = ((bf16[24,8,512]{2,0,1:T(8,128)(2,1)}), bf16[24,8,512]{2,0,1:T(8,128)(2,1)S(1)}, u32[]{:S(2)}, u32[]{:S(2)}) async-start(bf16[24,8,512]{2,0,1:T(8,128)(2,1)} %bitcast.89), calls=%async_computation.1 | async-start | bytes 393216 | tf_op jit(solution)/shard_map/all_to_all | solution.py:128
